TPU v7x, 32 devices: a whole 2x2x4 slice. The times are simulated.
32 devices in a mesh: space: 2 (over x), energy: 16 (over z, y, core).
Axes of the slice: x: 2, y: 2, z: 4, core: 2. Of those that a mesh axis runs over, the one named last changes fastest.
Arguments:
- lesser_in: bfloat16 [16, 2, 2, 256, 256], P('energy', 'space'), may hold values from -6 to 6
- retarded: bfloat16 [16, 2, 2, 256, 256], P('energy', 'space'), may hold values from -0.25 to 0.25
- coupling: bfloat16 [2, 2, 256, 256], P('space'), may hold values from -0.25 to 0.25
- interaction: bfloat16 [2, 32, 65536], P('space', None, 'energy'), may hold values from -1.5 to 1.5
Outputs:
- self_energy: bfloat16 [16, 2, 2, 256, 256], P('energy', 'space')
All inputs are finite; a program needn't handle non-finite values.
Results may differ from a plain program's by a relative error of at most 0.029.
Values may be sent and summed in bfloat16 or wider, within the bound.
A program may use at most 128 MiB of HBM per device.

v0:
```python
import math

import jax
import jax.numpy as jnp
from jax import lax
from jax.sharding import PartitionSpec as P


def product(left_real, left_imag, right_real, right_imag):
    real_part = jnp.dot(left_real, right_real, preferred_element_type=jnp.float32) - jnp.dot(
        left_imag, right_imag, preferred_element_type=jnp.float32
    )
    imag_part = jnp.dot(left_real, right_imag, preferred_element_type=jnp.float32) + jnp.dot(
        left_imag, right_real, preferred_element_type=jnp.float32
    )
    return (real_part, imag_part)


def phase_table(row_count, column_count, length):
    row_index = jnp.arange(row_count, dtype=jnp.int32)[:, None]
    column_index = jnp.arange(column_count, dtype=jnp.int32)[None, :]
    residue = row_index * column_index % length
    return residue.astype(jnp.float32) * (2.0 * math.pi / length)


def finish(spectrum_real, spectrum_imag, weights, energy_count, length):
    forward_scale = energy_count ** (-0.5)
    inverse_scale = length ** (-0.5)
    spectrum_real = spectrum_real * forward_scale
    spectrum_imag = spectrum_imag * forward_scale
    weight_values = weights.astype(jnp.float32)
    squared_real = (
        (spectrum_real * spectrum_real - spectrum_imag * spectrum_imag) * weight_values
    ).astype(jnp.bfloat16)
    squared_imag = (2.0 * spectrum_real * spectrum_imag * weight_values).astype(jnp.bfloat16)
    inverse_phase = phase_table(energy_count, length, length)
    inverse_real = jnp.cos(inverse_phase).astype(jnp.bfloat16)
    inverse_imag = jnp.sin(inverse_phase).astype(jnp.bfloat16)
    out_real, out_imag = product(inverse_real, inverse_imag, squared_real, squared_imag)
    return jnp.stack([out_real * inverse_scale, out_imag * inverse_scale], axis=1).astype(
        jnp.bfloat16
    )


def batched(pattern, former, latter):
    return jnp.einsum(pattern, former, latter, preferred_element_type=jnp.float32)


def local(lesser_in, retarded, coupling, interaction):
    local_count = lesser_in.shape[0]
    block_order = coupling.shape[-1]
    groups = lax.axis_size("energy")
    sections = lax.axis_size("space")
    energy_count = local_count * groups
    length = 2 * energy_count
    entry_width = block_order * block_order // groups
    resolvent_real = retarded[:, 0, 0]
    resolvent_imag = retarded[:, 0, 1]
    lesser_real = lesser_in[:, 0, 0]
    lesser_imag = lesser_in[:, 0, 1]
    coupling_real = coupling[0, 0]
    coupling_imag = coupling[0, 1]
    map_real = (
        batched("eij,jk->eik", resolvent_real, coupling_real)
        - batched("eij,jk->eik", resolvent_imag, coupling_imag)
    ).astype(jnp.bfloat16)
    map_imag = (
        batched("eij,jk->eik", resolvent_real, coupling_imag)
        + batched("eij,jk->eik", resolvent_imag, coupling_real)
    ).astype(jnp.bfloat16)
    half_real = (
        batched("eij,ejk->eik", resolvent_real, lesser_real)
        - batched("eij,ejk->eik", resolvent_imag, lesser_imag)
    ).astype(jnp.bfloat16)
    half_imag = (
        batched("eij,ejk->eik", resolvent_real, lesser_imag)
        + batched("eij,ejk->eik", resolvent_imag, lesser_real)
    ).astype(jnp.bfloat16)
    source_real = batched("eij,ekj->eik", half_real, resolvent_real) + batched(
        "eij,ekj->eik", half_imag, resolvent_imag
    )
    source_imag = batched("eij,ekj->eik", half_imag, resolvent_real) - batched(
        "eij,ekj->eik", half_real, resolvent_imag
    )
    forward_phase = phase_table(length, energy_count, length)
    forward_real = jnp.cos(forward_phase).astype(jnp.bfloat16)
    forward_imag = (-jnp.sin(forward_phase)).astype(jnp.bfloat16)
    padded = (local_count + sections - 1) // sections * sections
    extra = padded - local_count
    maps_all = jnp.pad(
        jnp.stack([map_real, map_imag], axis=1), ((0, extra), (0, 0), (0, 0), (0, 0))
    )
    sources_all = jnp.pad(
        jnp.stack([source_real, source_imag], axis=1), ((0, extra), (0, 0), (0, 0), (0, 0))
    )
    maps_here, sources_here = (
        lax.all_to_all(
            maps_all[:, None].astype(jnp.float32), "space", split_axis=0, concat_axis=1, tiled=True
        ).astype(jnp.bfloat16),
        lax.all_to_all(sources_all[:, None], "space", split_axis=0, concat_axis=1, tiled=True),
    )
    per_device = maps_here.shape[0]

    def link(carried, inputs_pair):
        step_map, step_source = inputs_pair
        carry_real = (
            batched("eij,ejk->eik", step_map[:, 0], carried[:, 0])
            - batched("eij,ejk->eik", step_map[:, 1], carried[:, 1])
        ).astype(jnp.bfloat16)
        carry_imag = (
            batched("eij,ejk->eik", step_map[:, 0], carried[:, 1])
            + batched("eij,ejk->eik", step_map[:, 1], carried[:, 0])
        ).astype(jnp.bfloat16)
        grown_real = batched("eij,ekj->eik", carry_real, step_map[:, 0]) + batched(
            "eij,ekj->eik", carry_imag, step_map[:, 1]
        )
        grown_imag = batched("eij,ekj->eik", carry_imag, step_map[:, 0]) - batched(
            "eij,ekj->eik", carry_real, step_map[:, 1]
        )
        fresh = jnp.stack(
            [step_source[:, 0] + grown_real, step_source[:, 1] + grown_imag], axis=1
        ).astype(jnp.bfloat16)
        return (fresh, fresh)

    start_block = jnp.zeros((per_device, 2, block_order, block_order), jnp.bfloat16)
    last_block, layers = lax.scan(
        link, start_block, (jnp.moveaxis(maps_here, 1, 0), jnp.moveaxis(sources_here, 1, 0))
    )
    greens = jnp.moveaxis(layers, 0, 1).reshape(per_device, sections, 2, block_order * block_order)
    homed = lax.all_to_all(
        lax.all_to_all(greens, "space", split_axis=1, concat_axis=0, tiled=True),
        "energy",
        split_axis=3,
        concat_axis=0,
        tiled=True,
    )
    entries = homed.reshape(groups, padded, 2, entry_width)[:, :local_count].reshape(
        energy_count, 2, entry_width
    )
    spectrum_real, spectrum_imag = product(forward_real, forward_imag, entries[:, 0], entries[:, 1])
    result = finish(spectrum_real, spectrum_imag, interaction[0], energy_count, length)
    returned = lax.all_to_all(result, "energy", split_axis=0, concat_axis=2, tiled=True)
    return returned.reshape(local_count, 1, 2, block_order, block_order)


def solution(mesh):
    in_specs = (
        P("energy", "space", None, None, None),
        P("energy", "space", None, None, None),
        P("space", None, None, None),
        P("space", None, "energy"),
    )
    out_specs = P("energy", "space", None, None, None)
    return jax.shard_map(local, mesh=mesh, in_specs=in_specs, out_specs=out_specs, check_vma=False)
```

profile of v0, /device:TPU:27, one launch (start us, length us, event | category | flops | bytes accessed | tf_op | source)
XLA Modules:
  0.0 316.5 jit_solution(13402352093027269052)
XLA Ops:
  0.0 1.1 fusion.41
  1.2 1.2 fusion.45
  2.3 1.2 fusion.31
  3.5 1.2 fusion.32
  4.6 0.8 fusion.40
  5.5 3.7 %all-to-all-start.1 = ((bf16[2,1,2,256,256]{4,3,2,1,0:T(8,128)(2,1)}), bf16[2,1,2,256,256]{4,3,2,1,0:T(8,128)(2,1)S(1)}, u32[]{:S(2)}, u32[]{:S(2)}) async-start(bf16[2,1,2,256,256]{4,3,2,1,0:T(8,128)(2,1)} %fusion.40), calls=%async_computation.1 | async-start | bytes 1048576 | tf_op jit(solution)/shard_map/all_to_all | solution.py:97
  9.2 1.1 fusion.47
  10.4 1.1 fusion.57
  11.5 1.2 fusion.28
  12.7 1.1 fusion.61
  13.8 1.2 fusion.27
  15.0 1.1 fusion.64
  16.1 1.1 fusion.25
  17.2 1.1 fusion.26
  18.4 1.0 fusion.33
  19.4 3.6 %all-to-all-start = ((f32[2,1,2,256,256]{4,3,2,1,0:T(8,128)}), f32[2,1,2,256,256]{4,3,2,1,0:T(8,128)S(1)}, u32[]{:S(2)}, u32[]{:S(2)}) async-start(f32[2,1,2,256,256]{4,3,2,1,0:T(8,128)} %fusion.33), calls=%async_computation | async-start | bytes 2097152 | tf_op jit(solution)/shard_map/all_to_all | solution.py:100
  23.0 11.9 %all-to-all-done = f32[2,1,2,256,256]{4,3,2,1,0:T(8,128)S(1)} async-done(((f32[2,1,2,256,256]{4,3,2,1,0:T(8,128)}), f32[2,1,2,256,256]{4,3,2,1,0:T(8,128)S(1)}, u32[]{:S(2)}, u32[]{:S(2)}) %all-to-all-start) | async-done | bytes 1048608 | tf_op jit(solution)/shard_map/all_to_all | solution.py:100
  34.9 3.7 %while.12 = (s32[]{:T(128)}, bf16[1,2,256,256]{3,2,1,0:T(8,128)(2,1)S(1)}, bf16[2,1,2,256,256]{4,3,2,1,0:T(8,128)(2,1)S(1)}, f32[2,1,2,256,256]{4,3,2,1,0:T(8,12...) while((s32[]{:T(128)}, bf16[1,2,256,256]{3,2,1,0:T(8,128)(2,1)S(1)}, ...), condition=%wide.region_1.2_spmd, body=%wide.region_0.1_spmd.sunk | while | flops 269746176 | bytes 7864409 | solution.py:126
  35.1 0.2 fusion.175
  35.3 0.2 fusion.177
  35.5 0.2 fusion.171
  35.7 0.2 fusion.172
  35.9 0.2 fusion.173
  36.2 0.2 fusion.178
  36.4 0.2 fusion.176
  37.0 0.2 fusion.175
  37.2 0.2 fusion.177
  37.6 0.2 fusion.172
  37.8 0.2 fusion.173
  38.0 0.2 fusion.178
  38.3 0.2 fusion.176
  38.8 9.0 %all_to_all.60 = bf16[1,2,2,65536]{3,2,0,1:T(2,128)(2,1)S(1)} all-to-all(bf16[1,2,2,65536]{3,2,0,1:T(2,128)(2,1)S(1)} %reshape_transpose.3), channel_id=1, replica_groups=mesh['space'=2,'energy'=16] {'space'}, dimensions={1} | all-to-all | bytes 1048576 | tf_op jit(solution)/shard_map/all_to_all | solution.py:131
  47.7 50.9 %copy.13 = bf16[2,1,2,65536]{2,0,1,3:T(2,128)(2,1)} copy(bf16[2,1,2,65536]{3,2,0,1:T(2,128)(2,1)S(1)} %bitcast.204) | data formatting | bytes 1048576 | tf_op jit(solution)/shard_map/all_to_all | solution.py:131
  98.6 61.2 %reshape.243 = bf16[16,2,8192]{2,1,0:T(2,128)(2,1)S(1)} reshape(bf16[65536,1,2,2]{3,2,1,0:T(2,128)(2,1)} %bitcast.198) | data formatting | bytes 1048576
  159.8 20.2 %all_to_all.61 = bf16[16,2,8192]{2,1,0:T(2,128)(2,1)S(1)} all-to-all(bf16[16,2,8192]{2,1,0:T(2,128)(2,1)S(1)} %reshape.243), channel_id=1, replica_groups=mesh['space'=2,'energy'=16] {'energy'}, dimensions={0} | all-to-all | bytes 1048576 | tf_op jit(solution)/shard_map/all_to_all | solution.py:130
  179.9 73.4 %reshape.244 = bf16[65536,1,2,2]{3,2,1,0:T(2,128)(2,1)} reshape(bf16[16,2,8192]{2,1,0:T(2,128)(2,1)S(1)} %all_to_all.61) | data formatting | bytes 1048576
  253.3 46.6 %copy.17 = bf16[2,1,2,16,4096]{4,3,2,0,1:T(8,128)(2,1)S(1)} copy(bf16[2,1,2,16,4096]{2,0,4,3,1:T(2,128)(2,1)} %bitcast.199) | data formatting | bytes 1048576 | tf_op jit(solution)/shard_map/all_to_all | solution.py:130
  299.9 0.3 fusion.68
  300.2 0.3 fusion.67
  300.5 0.3 convolution_subtract_fusion.2
  300.8 0.4 fusion.36
  301.2 0.2 fusion.102
  301.4 0.2 fusion.101
  301.6 0.2 fusion.24
  301.8 0.2 fusion.23
  302.1 0.3 copy.15
  302.4 13.1 %all_to_all.62 = bf16[16,2,4096]{2,1,0:T(2,128)(2,1)S(1)} all-to-all(bf16[16,2,4096]{2,1,0:T(2,128)(2,1)S(1)} %copy.15), channel_id=1, replica_groups=mesh['space'=2,'energy'=16] {'energy'}, dimensions={0} | all-to-all | bytes 524288 | tf_op jit(solution)/shard_map/all_to_all | solution.py:142
  315.7 0.8 reshape.240
  (20 shorter events, 1.2 us)
Async XLA Ops:
  5.5 13.9 %all-to-all-start.1 = ((bf16[2,1,2,256,256]{4,3,2,1,0:T(8,128)(2,1)}), bf16[2,1,2,256,256]{4,3,2,1,0:T(8,128)(2,1)S(1)}, u32[]{:S(2)}, u32[]{:S(2)}) async-start(bf16[2,1,2,256,256]{4,3,2,1,0:T(8,128)(2,1)} %fusion.40), calls=%async_computation.1 | async-start | bytes 1048576 | tf_op jit(solution)/shard_map/all_to_all | solution.py:97
  19.4 15.4 %all-to-all-start = ((f32[2,1,2,256,256]{4,3,2,1,0:T(8,128)}), f32[2,1,2,256,256]{4,3,2,1,0:T(8,128)S(1)}, u32[]{:S(2)}, u32[]{:S(2)}) async-start(f32[2,1,2,256,256]{4,3,2,1,0:T(8,128)} %fusion.33), calls=%async_computation | async-start | bytes 2097152 | tf_op jit(solution)/shard_map/all_to_all | solution.py:100
  179.9 120.8 %copy-start = (bf16[1,32,4096]{2,1,0:T(8,128)(2,1)S(1)}, bf16[1,32,4096]{2,1,0:T(8,128)(2,1)}, u32[]{:S(2)}) copy-start(bf16[1,32,4096]{2,1,0:T(8,128)(2,1)} %param.9) | copy-start | bytes 786436
where the time goes:
time: 323 us; the launch traced here: 317 us
  local copies, waits for them, and re-layouts  234 us (72%)
  blocking collectives  42.3 us (13%)
  matrix products  19.1 us (6%)
  waiting for transfers between devices  11.9 us (4%)
  starting transfers between devices  7.32 us (2%)
    unnamed x4, local copies, waits for them, and re-layouts  135 us
    all_to_all x1, local copies, waits for them, and re-layouts, local(): lax.all_to_all(greens, 'space', split_axis=1, concat_axis=0, tiled=True)  50.9 us
    all_to_all x1, local copies, waits for them, and re-layouts, local(): lax.all_to_all(lax.all_to_all(greens, 'space', split_axis=1, concat_axis=...  46.6 us
    all_to_all x1, blocking collectives, local(): lax.all_to_all(lax.all_to_all(greens, 'space', split_axis=1, concat_axis=...  20.2 us
    dot_general x28, matrix products, batched(): jnp.einsum(pattern, former, latter, preferred_element_type=jnp.float32)  17 us
    all_to_all x1, blocking collectives, local(): lax.all_to_all(result, 'energy', split_axis=0, concat_axis=2, tiled=True)  13.1 us
    all_to_all x1, waiting for transfers between devices, local(): lax.all_to_all(sources_all[:, None], 'space', split_axis=0, concat_axis=1...  11.9 us
    all_to_all x1, blocking collectives, local(): lax.all_to_all(greens, 'space', split_axis=1, concat_axis=0, tiled=True)  8.97 us
  transfers between devices with their start and end apart: 2, of which 1 were waited for; matrix products, arithmetic and copies ran while one was open for 3% of the time, Pallas kernels for 0%

commit v1 on v0

v1 whole, which is shorter than its diff:
```python
import functools
import math

import jax
import jax.numpy as jnp
import numpy as np
from jax import lax
from jax.experimental import pallas as pl
from jax.experimental.pallas import tpu as pltpu
from jax.sharding import PartitionSpec as P

MESH = pl.DeviceIdType.MESH
ANY = pl.BlockSpec(memory_space=pl.ANY)


def phase_parts(row_count, column_count, length):
    residue = np.arange(row_count)[:, None] * np.arange(column_count)[None, :] % length
    phase = residue * (2.0 * math.pi / length)
    return np.cos(phase), np.sin(phase)


def forward_matrix(energy_count, length, rows):
    cosine, sine = phase_parts(length, energy_count, length)
    small = np.array([[cosine, sine], [-sine, cosine]])
    full = np.einsum("pqfe,rs->rpfeqs", small, np.eye(rows))
    return full.reshape(rows * 2 * length, energy_count * 2 * rows).astype(jnp.bfloat16)


def inverse_matrix(energy_count, length, rows):
    cosine, sine = phase_parts(energy_count, length, length)
    small = np.array([[cosine, -sine], [sine, cosine]])
    full = np.einsum("pqef,rs->eprsqf", small, np.eye(rows))
    return full.reshape(energy_count * 2 * rows, rows * 2 * length).astype(jnp.bfloat16)


def dot(left, right):
    return jnp.dot(left, right, preferred_element_type=jnp.float32)


def dot_t(left, right):
    return lax.dot_general(
        left, right, (((1,), (1,)), ((), ())), preferred_element_type=jnp.float32
    )


def kernel(
    sections, groups, rows, length, pieces,
    lesser_hbm, retarded_hbm, coupling_hbm, interaction_hbm, forward_hbm, inverse_hbm,
    out_hbm,
    lesser, retarded, coupling, interaction, forward, inverse,
    total, maps, green, before, homing, homed, weighted, leaving,
    load_sem, hop_send, hop_recv, go_send, go_recv, back_send, back_recv, own_sem,
):
    section = lax.axis_index("space")
    me = lax.axis_index("energy")
    order = green.shape[-1]
    width = order // pieces

    barrier = pltpu.get_barrier_semaphore()
    for step in range(1, groups):
        peer = lax.rem(me + step, groups)
        pl.semaphore_signal(barrier, inc=1, device_id={"energy": peer}, device_id_type=MESH)

    @pl.when(section > 0)
    def _():
        pl.semaphore_signal(barrier, inc=1, device_id={"space": section - 1}, device_id_type=MESH)

    @pl.when(section < sections - 1)
    def _():
        pl.semaphore_signal(barrier, inc=1, device_id={"space": section + 1}, device_id_type=MESH)

    loads = []
    for at, (source, target) in enumerate((
        (retarded_hbm.at[0, 0], retarded),
        (lesser_hbm.at[0, 0], lesser),
        (coupling_hbm.at[0], coupling),
        (interaction_hbm.at[0], interaction),
        (forward_hbm, forward),
        (inverse_hbm, inverse),
    )):
        load = pltpu.make_async_copy(source, target, load_sem.at[at])
        load.start()
        loads.append(load)

    loads[0].wait()
    loads[1].wait()
    r_re, r_im = retarded[0], retarded[1]
    l_re, l_im = lesser[0], lesser[1]
    half_re = (dot(r_re, l_re) - dot(r_im, l_im)).astype(jnp.bfloat16)
    half_im = (dot(r_re, l_im) + dot(r_im, l_re)).astype(jnp.bfloat16)
    total[0] = dot_t(half_re, r_re) + dot_t(half_im, r_im)
    total[1] = dot_t(half_im, r_re) - dot_t(half_re, r_im)

    pl.semaphore_wait(
        barrier,
        groups - 1 + jnp.where(section > 0, 1, 0) + jnp.where(section < sections - 1, 1, 0),
    )
    loads[2].wait()

    def hop(piece, target):
        columns = pl.ds(piece * width, width)
        return pltpu.make_async_remote_copy(
            src_ref=green.at[:, :, columns],
            dst_ref=before.at[:, :, columns],
            send_sem=hop_send.at[piece],
            recv_sem=hop_recv.at[piece],
            device_id={"space": target},
            device_id_type=MESH,
        )

    @pl.when(section > 0)
    def _():
        c_re, c_im = coupling[0], coupling[1]
        maps[0] = (dot(r_re, c_re) - dot(r_im, c_im)).astype(jnp.bfloat16)
        maps[1] = (dot(r_re, c_im) + dot(r_im, c_re)).astype(jnp.bfloat16)
        for piece in range(pieces):
            hop(piece, section - 1).wait_recv()
            part = slice(piece * width, (piece + 1) * width)
            b_re, b_im = before[0, :, part], before[1, :, part]
            m_re, m_im = maps[0], maps[1]
            k_re = (dot(m_re, b_re) - dot(m_im, b_im)).astype(jnp.bfloat16)
            k_im = (dot(m_re, b_im) + dot(m_im, b_re)).astype(jnp.bfloat16)
            n_re, n_im = maps[0, :, part], maps[1, :, part]
            total[0] += dot_t(k_re, n_re) + dot_t(k_im, n_im)
            total[1] += dot_t(k_im, n_re) - dot_t(k_re, n_im)

    @pl.when(section < sections - 1)
    def _():
        green[...] = total[...].astype(jnp.bfloat16)
        for piece in range(pieces):
            hop(piece, section + 1).start()

    homing[...] = jnp.concatenate(
        [total[part].reshape(groups, rows, order) for part in range(2)], axis=1
    ).astype(jnp.bfloat16)

    def go(peer, slot):
        return pltpu.make_async_remote_copy(
            src_ref=homing.at[peer],
            dst_ref=homed.at[slot],
            send_sem=go_send.at[peer],
            recv_sem=go_recv.at[slot],
            device_id={"energy": peer},
            device_id_type=MESH,
        )

    def back(peer, slot):
        return pltpu.make_async_remote_copy(
            src_ref=leaving.at[peer],
            dst_ref=out_hbm.at[slot],
            send_sem=back_send.at[peer],
            recv_sem=back_recv.at[slot],
            device_id={"energy": peer},
            device_id_type=MESH,
        )

    peers = [lax.rem(me + step, groups) for step in range(1, groups)]
    for peer in peers:
        go(peer, me).start()
    own = pltpu.make_async_copy(homing.at[me], homed.at[me], own_sem.at[0])
    own.start()
    for load in loads[3:]:
        load.wait()
    own.wait()
    for peer in peers:
        go(peer, peer).wait_recv()

    entries = homed[...]
    if 2 * rows % 16:
        entries = entries.astype(jnp.float32)
    entries = entries.reshape(groups * 2 * rows, order).astype(jnp.bfloat16)
    stride = 2 * length
    chunk = max(1, order // stride)
    for first in range(0, rows, chunk):
        spectrum = dot(forward[first * stride:(first + chunk) * stride, :], entries)
        spectrum = spectrum * groups ** -0.5
        for at in range(chunk):
            row = first + at
            s_re = spectrum[at * stride:at * stride + length]
            s_im = spectrum[at * stride + length:(at + 1) * stride]
            weight = interaction[:, row * order:(row + 1) * order].astype(jnp.float32)
            weighted[row * stride:row * stride + length, :] = (
                (s_re * s_re - s_im * s_im) * weight
            ).astype(jnp.bfloat16)
            weighted[row * stride + length:(row + 1) * stride, :] = (
                2.0 * s_re * s_im * weight
            ).astype(jnp.bfloat16)
    result = dot(inverse[...], weighted[...]) * length ** -0.5
    leaving[...] = result.reshape(groups, 2 * rows, order).astype(jnp.bfloat16)

    for peer in peers:
        back(peer, me).start()
    own = pltpu.make_async_copy(leaving.at[me], out_hbm.at[me], own_sem.at[1])
    own.start()
    for peer in peers:
        go(peer, me).wait_send()

    @pl.when(section < sections - 1)
    def _():
        for piece in range(pieces):
            hop(piece, section + 1).wait_send()

    own.wait()
    for peer in peers:
        back(peer, me).wait_send()
    for peer in peers:
        back(peer, peer).wait_recv()


def local(lesser_in, retarded, coupling, interaction):
    order = coupling.shape[-1]
    groups = lax.axis_size("energy")
    sections = lax.axis_size("space")
    length = interaction.shape[1]
    rows = order // groups
    pieces = 2
    assert lesser_in.shape[0] == 1 and coupling.shape[0] == 1
    forward = jnp.asarray(forward_matrix(groups, length, rows))
    inverse = jnp.asarray(inverse_matrix(groups, length, rows))
    low, wide = jnp.bfloat16, jnp.float32
    dma = pltpu.SemaphoreType.DMA
    returned = pl.pallas_call(
        functools.partial(kernel, sections, groups, rows, length, pieces),
        out_shape=jax.ShapeDtypeStruct((groups, 2 * rows, order), low),
        in_specs=[ANY] * 6,
        out_specs=ANY,
        scratch_shapes=[
            pltpu.VMEM((2, order, order), low),
            pltpu.VMEM((2, order, order), low),
            pltpu.VMEM((2, order, order), low),
            pltpu.VMEM(interaction.shape[1:], low),
            pltpu.VMEM(forward.shape, low),
            pltpu.VMEM(inverse.shape, low),
            pltpu.VMEM((2, order, order), wide),
            pltpu.VMEM((2, order, order), low),
            pltpu.VMEM((2, order, order), low),
            pltpu.VMEM((2, order, order), low),
            pltpu.VMEM((groups, 2 * rows, order), low),
            pltpu.VMEM((groups, 2 * rows, order), low),
            pltpu.VMEM((rows * 2 * length, order), low),
            pltpu.VMEM((groups, 2 * rows, order), low),
            dma((6,)),
            dma((pieces,)),
            dma((pieces,)),
            dma((groups,)),
            dma((groups,)),
            dma((groups,)),
            dma((groups,)),
            dma((2,)),
        ],
        compiler_params=pltpu.CompilerParams(
            collective_id=0, has_side_effects=True
        ),
    )(lesser_in, retarded, coupling, interaction, forward, inverse)
    returned = returned.reshape(groups, 2, rows, order).transpose(1, 0, 2, 3)
    return returned.reshape(1, 1, 2, order, order)


def solution(mesh):
    in_specs = (
        P("energy", "space", None, None, None),
        P("energy", "space", None, None, None),
        P("space", None, None, None),
        P("space", None, "energy"),
    )
    out_specs = P("energy", "space", None, None, None)
    return jax.shard_map(local, mesh=mesh, in_specs=in_specs, out_specs=out_specs, check_vma=False)
```

time: 323 us -> 28.5 us (0.09); the launches traced: 317 us -> 28.3 us
  local copies, waits for them, and re-layouts: 234 us -> 1.67 us
  blocking collectives: 42.3 us -> 0 us
  Pallas kernels: 0 us -> 26.6 us
  matrix products: 19.1 us -> 0 us
  waiting for transfers between devices: 11.9 us -> 0 us
  starting transfers between devices: 7.32 us -> 0 us
    unnamed x4 -> x0, local copies, waits for them, and re-layouts: 135 us -> none
    all_to_all x3 -> x0, local copies, waits for them, and re-layouts: 97.6 us -> none  [the longest x1 50.9 us: local(): lax.all_to_all(greens, 'space', split_axis=1, concat_axis=0, tiled=True)]
    all_to_all x3 -> x0, blocking collectives: 42.3 us -> none  [the longest x1 20.2 us: local(): lax.all_to_all(lax.all_to_all(greens, 'space', split_axis=1, concat_axis=...]
    pallas_call x0 -> x1, Pallas kernels: none -> 26.6 us  [local(): pl.pallas_call(functools.partial(kernel, sections, groups, rows, length,...]
    dot_general x36 -> x0, matrix products: 19.1 us -> none  [the longest x28 17 us: batched(): jnp.einsum(pattern, former, latter, preferred_element_type=jnp.float32)]
    all_to_all x2 -> x0, waiting for transfers between devices: 11.9 us -> none  [the longest x1 11.9 us: local(): lax.all_to_all(sources_all[:, None], 'space', split_axis=0, concat_axis=1...]
    all_to_all x2 -> x0, starting transfers between devices: 7.32 us -> none  [the longest x1 3.73 us: local(): lax.all_to_all(maps_all[:, None].astype(jnp.float32), 'space', split_axis...]
  transfers between devices with their start and end apart: 2 -> 0, of which waited for: 1 -> 0; matrix products, arithmetic and copies ran while one was open for 3% -> 0% of each run, Pallas kernels for 0% -> 0%
where the time goes in v1:
time: 28.5 us; the launch traced here: 28.3 us
  Pallas kernels  26.6 us (93%)
  local copies, waits for them, and re-layouts  1.67 us (6%)
    pallas_call x1, Pallas kernels, local(): pl.pallas_call(functools.partial(kernel, sections, groups, rows, length,...  26.6 us
    transpose x1, local copies, waits for them, and re-layouts, local(): returned = returned.reshape(groups, 2, rows, order).transpose(1, 0, 2, 3)  1.67 us

profile of v1, /device:TPU:27, one launch (start us, length us, event | category | flops | bytes accessed | tf_op | source)
XLA Modules:
  0.0 28.3 jit_solution(6708081753397798487)
XLA Ops:
  0.0 26.6 %shard_map.64 = bf16[16,32,256]{2,1,0:T(8,128)(2,1)} custom-call(bf16[1,1,2,256,256]{4,3,2,1,0:T(8,128)(2,1)} %lesser_hbm.1, bf16[1,1,2,256,256]{4,3,2,1,0:T(8,128)(2,1)} %retarded_hbm.1, bf16[1,2,256,256]{3,2,1,0:T(8,128)(2,1)} %coupling_hbm.1, bf16[1,32,4096]{2,1,0:T(8,128)(2,1)} %interaction_hbm.1, bf16[1024,512]{1,0:T(8,128)(2,1)} %constant.4.clone.forward_hbm, ...), custom_call_target="tpu_custom_call" | custom-call | tf_op jit(solution)/shard_map/pallas_call | solution.py:222
  26.6 1.7 %copy.7 = bf16[2,16,16,256]{3,2,1,0:T(8,128)(2,1)} copy(bf16[2,16,16,256]{3,2,0,1:T(8,128)(2,1)} %bitcast.4) | data formatting | bytes 524288 | tf_op jit(solution)/shard_map/transpose | solution.py:255

commit v2 on v1

--- a/solution.py
+++ b/solution.py
@@ -44,7 +44,7 @@
 
 
 def kernel(
-    sections, groups, rows, length, pieces,
+    sections, groups, rows, length, pieces, parts,
     lesser_hbm, retarded_hbm, coupling_hbm, interaction_hbm, forward_hbm, inverse_hbm,
     out_hbm,
     lesser, retarded, coupling, interaction, forward, inverse,
@@ -130,81 +130,96 @@
         for piece in range(pieces):
             hop(piece, section + 1).start()
 
-    homing[...] = jnp.concatenate(
-        [total[part].reshape(groups, rows, order) for part in range(2)], axis=1
-    ).astype(jnp.bfloat16)
-
-    def go(peer, slot):
+    share = rows // parts
+    for part in range(parts):
+        homing[part] = jnp.concatenate(
+            [
+                total[side].reshape(groups, parts, share, order)[:, part]
+                for side in range(2)
+            ],
+            axis=1,
+        ).astype(jnp.bfloat16)
+
+    def go(part, peer, slot):
         return pltpu.make_async_remote_copy(
-            src_ref=homing.at[peer],
-            dst_ref=homed.at[slot],
-            send_sem=go_send.at[peer],
-            recv_sem=go_recv.at[slot],
+            src_ref=homing.at[part, peer],
+            dst_ref=homed.at[part, slot],
+            send_sem=go_send.at[part, peer],
+            recv_sem=go_recv.at[part, slot],
             device_id={"energy": peer},
             device_id_type=MESH,
         )
 
-    def back(peer, slot):
+    def back(part, peer, slot):
         return pltpu.make_async_remote_copy(
-            src_ref=leaving.at[peer],
-            dst_ref=out_hbm.at[slot],
-            send_sem=back_send.at[peer],
-            recv_sem=back_recv.at[slot],
+            src_ref=leaving.at[part, peer],
+            dst_ref=out_hbm.at[slot, part],
+            send_sem=back_send.at[part, peer],
+            recv_sem=back_recv.at[part, slot],
             device_id={"energy": peer},
             device_id_type=MESH,
         )
 
     peers = [lax.rem(me + step, groups) for step in range(1, groups)]
-    for peer in peers:
-        go(peer, me).start()
-    own = pltpu.make_async_copy(homing.at[me], homed.at[me], own_sem.at[0])
-    own.start()
+    kept = []
+    for part in range(parts):
+        for peer in peers:
+            go(part, peer, me).start()
+        own = pltpu.make_async_copy(homing.at[part, me], homed.at[part, me], own_sem.at[0, part])
+        own.start()
+        kept.append(own)
     for load in loads[3:]:
         load.wait()
-    own.wait()
-    for peer in peers:
-        go(peer, peer).wait_recv()
-
-    entries = homed[...]
-    if 2 * rows % 16:
-        entries = entries.astype(jnp.float32)
-    entries = entries.reshape(groups * 2 * rows, order).astype(jnp.bfloat16)
+
     stride = 2 * length
     chunk = max(1, order // stride)
-    for first in range(0, rows, chunk):
-        spectrum = dot(forward[first * stride:(first + chunk) * stride, :], entries)
-        spectrum = spectrum * groups ** -0.5
-        for at in range(chunk):
-            row = first + at
-            s_re = spectrum[at * stride:at * stride + length]
-            s_im = spectrum[at * stride + length:(at + 1) * stride]
-            weight = interaction[:, row * order:(row + 1) * order].astype(jnp.float32)
-            weighted[row * stride:row * stride + length, :] = (
-                (s_re * s_re - s_im * s_im) * weight
-            ).astype(jnp.bfloat16)
-            weighted[row * stride + length:(row + 1) * stride, :] = (
-                2.0 * s_re * s_im * weight
-            ).astype(jnp.bfloat16)
-    result = dot(inverse[...], weighted[...]) * length ** -0.5
-    leaving[...] = result.reshape(groups, 2 * rows, order).astype(jnp.bfloat16)
-
-    for peer in peers:
-        back(peer, me).start()
-    own = pltpu.make_async_copy(leaving.at[me], out_hbm.at[me], own_sem.at[1])
-    own.start()
-    for peer in peers:
-        go(peer, me).wait_send()
+    returns = []
+    for part in range(parts):
+        kept[part].wait()
+        for peer in peers:
+            go(part, peer, peer).wait_recv()
+        entries = homed[part]
+        if 2 * share % 16:
+            entries = entries.astype(jnp.float32)
+        entries = entries.reshape(groups * 2 * share, order).astype(jnp.bfloat16)
+        for first in range(0, share, chunk):
+            spectrum = dot(forward[first * stride:(first + chunk) * stride, :], entries)
+            spectrum = spectrum * groups ** -0.5
+            for at in range(chunk):
+                row = first + at
+                s_re = spectrum[at * stride:at * stride + length]
+                s_im = spectrum[at * stride + length:(at + 1) * stride]
+                entry = (part * share + row) * order
+                weight = interaction[:, entry:entry + order].astype(jnp.float32)
+                weighted[row * stride:row * stride + length, :] = (
+                    (s_re * s_re - s_im * s_im) * weight
+                ).astype(jnp.bfloat16)
+                weighted[row * stride + length:(row + 1) * stride, :] = (
+                    2.0 * s_re * s_im * weight
+                ).astype(jnp.bfloat16)
+        result = dot(inverse[...], weighted[...]) * length ** -0.5
+        leaving[part] = result.reshape(groups, 2 * share, order).astype(jnp.bfloat16)
+        for peer in peers:
+            back(part, peer, me).start()
+        own = pltpu.make_async_copy(leaving.at[part, me], out_hbm.at[me, part], own_sem.at[1, part])
+        own.start()
+        returns.append(own)
+
+    for part in range(parts):
+        for peer in peers:
+            go(part, peer, me).wait_send()
 
     @pl.when(section < sections - 1)
     def _():
         for piece in range(pieces):
             hop(piece, section + 1).wait_send()
 
-    own.wait()
-    for peer in peers:
-        back(peer, me).wait_send()
-    for peer in peers:
-        back(peer, peer).wait_recv()
+    for part in range(parts):
+        returns[part].wait()
+        for peer in peers:
+            back(part, peer, me).wait_send()
+        for peer in peers:
+            back(part, peer, peer).wait_recv()
 
 
 def local(lesser_in, retarded, coupling, interaction):
@@ -214,14 +229,16 @@
     length = interaction.shape[1]
     rows = order // groups
     pieces = 2
+    parts = 2 if rows % 16 == 0 else 1
+    share = rows // parts
     assert lesser_in.shape[0] == 1 and coupling.shape[0] == 1
-    forward = jnp.asarray(forward_matrix(groups, length, rows))
-    inverse = jnp.asarray(inverse_matrix(groups, length, rows))
+    forward = jnp.asarray(forward_matrix(groups, length, share))
+    inverse = jnp.asarray(inverse_matrix(groups, length, share))
     low, wide = jnp.bfloat16, jnp.float32
     dma = pltpu.SemaphoreType.DMA
     returned = pl.pallas_call(
-        functools.partial(kernel, sections, groups, rows, length, pieces),
-        out_shape=jax.ShapeDtypeStruct((groups, 2 * rows, order), low),
+        functools.partial(kernel, sections, groups, rows, length, pieces, parts),
+        out_shape=jax.ShapeDtypeStruct((groups, parts, 2 * share, order), low),
         in_specs=[ANY] * 6,
         out_specs=ANY,
         scratch_shapes=[
@@ -235,24 +252,24 @@
             pltpu.VMEM((2, order, order), low),
             pltpu.VMEM((2, order, order), low),
             pltpu.VMEM((2, order, order), low),
-            pltpu.VMEM((groups, 2 * rows, order), low),
-            pltpu.VMEM((groups, 2 * rows, order), low),
-            pltpu.VMEM((rows * 2 * length, order), low),
-            pltpu.VMEM((groups, 2 * rows, order), low),
+            pltpu.VMEM((parts, groups, 2 * share, order), low),
+            pltpu.VMEM((parts, groups, 2 * share, order), low),
+            pltpu.VMEM((share * 2 * length, order), low),
+            pltpu.VMEM((parts, groups, 2 * share, order), low),
             dma((6,)),
             dma((pieces,)),
             dma((pieces,)),
-            dma((groups,)),
-            dma((groups,)),
-            dma((groups,)),
-            dma((groups,)),
-            dma((2,)),
+            dma((parts, groups)),
+            dma((parts, groups)),
+            dma((parts, groups)),
+            dma((parts, groups)),
+            dma((2, parts)),
         ],
         compiler_params=pltpu.CompilerParams(
             collective_id=0, has_side_effects=True
         ),
     )(lesser_in, retarded, coupling, interaction, forward, inverse)
-    returned = returned.reshape(groups, 2, rows, order).transpose(1, 0, 2, 3)
+    returned = returned.reshape(groups, parts, 2, share, order).transpose(2, 0, 1, 3, 4)
     return returned.reshape(1, 1, 2, order, order)
 
 

time: 28.5 us -> 28.3 us (level)
  Pallas kernels: 26.6 us -> 26.2 us
    pallas_call x1, Pallas kernels: 26.6 us -> 26.2 us  [local(): pl.pallas_call(functools.partial(kernel, sections, groups, rows, length,...]
where the time goes in v2:
time: 28.3 us; the launch traced here: 27.8 us
  Pallas kernels  26.2 us (93%)
  local copies, waits for them, and re-layouts  1.67 us (6%)
    pallas_call x1, Pallas kernels, local(): pl.pallas_call(functools.partial(kernel, sections, groups, rows, length,...  26.2 us
    transpose x1, local copies, waits for them, and re-layouts, local(): returned.reshape(groups, parts, 2, share, order).transpose(2, 0, 1, 3, 4)  1.67 us

profile of v2, /device:TPU:27, one launch (start us, length us, event | category | flops | bytes accessed | tf_op | source)
XLA Modules:
  0.0 27.8 jit_solution(5093067257417413944)
XLA Ops:
  0.0 26.2 %shard_map.64 = bf16[16,2,16,256]{3,2,1,0:T(8,128)(2,1)} custom-call(bf16[1,1,2,256,256]{4,3,2,1,0:T(8,128)(2,1)} %lesser_hbm.1, bf16[1,1,2,256,256]{4,3,2,1,0:T(8,128)(2,1)} %retarded_hbm.1, bf16[1,2,256,256]{3,2,1,0:T(8,128)(2,1)} %coupling_hbm.1, bf16[1,32,4096]{2,1,0:T(8,128)(2,1)} %interaction_hbm.1, bf16[512,256]{1,0:T(8,128)(2,1)} %constant.4.clone.forward_hbm, ...), custom_call_target="tpu_custom_call" | custom-call | tf_op jit(solution)/shard_map/pallas_call | solution.py:239
  26.2 1.7 %copy.7 = bf16[2,16,2,8,256]{4,3,2,1,0:T(8,128)(2,1)} copy(bf16[2,16,2,8,256]{4,3,0,2,1:T(8,128)(2,1)} %bitcast.4) | data formatting | bytes 524288 | tf_op jit(solution)/shard_map/transpose | solution.py:272

commit v3 on v2

--- a/solution.py
+++ b/solution.py
@@ -160,7 +160,8 @@
             device_id_type=MESH,
         )
 
-    peers = [lax.rem(me + step, groups) for step in range(1, groups)]
+    far_first = sorted(range(1, groups), key=lambda step: -min(step, groups - step))
+    peers = [lax.rem(me + step, groups) for step in far_first]
     kept = []
     for part in range(parts):
         for peer in peers:

time: 28.3 us -> 29.3 us (1.035)
  the two profiles are of different devices: /device:TPU:27 before, /device:TPU:2 now
where the time goes in v3:
time: 29.3 us; the launch traced here: 29.1 us
  Pallas kernels  27.5 us (94%)
  local copies, waits for them, and re-layouts  1.67 us (6%)
    pallas_call x1, Pallas kernels, local(): pl.pallas_call(functools.partial(kernel, sections, groups, rows, length,...  27.5 us
    transpose x1, local copies, waits for them, and re-layouts, local(): returned.reshape(groups, parts, 2, share, order).transpose(2, 0, 1, 3, 4)  1.67 us

profile of v3, /device:TPU:2, one launch (start us, length us, event | category | flops | bytes accessed | tf_op | source)
XLA Modules:
  0.0 29.1 jit_solution(17012158461957757372)
XLA Ops:
  0.0 27.5 %shard_map.64 = bf16[16,2,16,256]{3,2,1,0:T(8,128)(2,1)} custom-call(bf16[1,1,2,256,256]{4,3,2,1,0:T(8,128)(2,1)} %lesser_hbm.1, bf16[1,1,2,256,256]{4,3,2,1,0:T(8,128)(2,1)} %retarded_hbm.1, bf16[1,2,256,256]{3,2,1,0:T(8,128)(2,1)} %coupling_hbm.1, bf16[1,32,4096]{2,1,0:T(8,128)(2,1)} %interaction_hbm.1, bf16[512,256]{1,0:T(8,128)(2,1)} %constant.4.clone.forward_hbm, ...), custom_call_target="tpu_custom_call" | custom-call | tf_op jit(solution)/shard_map/pallas_call | solution.py:240
  27.5 1.7 %copy.7 = bf16[2,16,2,8,256]{4,3,2,1,0:T(8,128)(2,1)} copy(bf16[2,16,2,8,256]{4,3,0,2,1:T(8,128)(2,1)} %bitcast.4) | data formatting | bytes 524288 | tf_op jit(solution)/shard_map/transpose | solution.py:273
